TPU v7x, 32 devices: a whole 2x2x4 slice. The times are simulated.
32 devices in a mesh: rep: 2 (over x), shard: 16 (over z, y, core).
Axes of the slice: x: 2, y: 2, z: 4, core: 2. Of those that a mesh axis runs over, the one named last changes fastest.
Arguments:
- features: float32 [16384, 256], P(('rep', 'shard')), may hold values from -6 to 6
- seed_self: float32 [4096, 256], P(('rep', 'shard')), may hold values from -6 to 6
- hub_ids: int32 [4096], P(('rep', 'shard')), may hold values from 0 to 511
- requests: int32 [512, 32], P(('rep', 'shard')), may hold values from 0 to 511
- counts: int32 [512], P(('rep', 'shard')), may hold values from 1 to 32, as said below
- neighbors: int32 [4096, 15], P(('rep', 'shard')), may hold values from 0 to 767
- weight: float32 [256, 256], replicated, may hold values from -1 to 1
- out_bias: float32 [256], replicated, may hold values from -4 to 4
Outputs:
- embedded: float32 [4096, 256], P(('rep', 'shard'))
Inputs may be any that keep to these rules, and one draw needn't show every extreme that they name: `hub_ids`: offsets into the block of features of the same device. `requests`: row d of a device's lists holds offsets into the block of features of the device at shard index d with the same rep index; empty slots hold offsets too. counts[r, s, d] slots of the list from shard index s to shard index d are live, the first ones; for every rep index some destination has 32 live slots from every source. `neighbors`: A code below 256 names a row of the device's hub cache; a code 256 + d * 32 + c names slot c of the device's list to shard index d, and counts only where that slot is live.
All inputs are finite; a program needn't handle non-finite values.
Results may differ from a plain program's by a relative error of at most 0.0003.
Values sent between devices are 32-bit elements; how exact they have to be, the bound alone decides.
No kernel may reach another device: no remote copies, remote signals or barrier semaphores. Data moves between devices by JAX's collectives and lax.ppermute only.
A program may use at most 64 MiB of HBM per device.

v0:
```python
import math

import jax
import jax.numpy as jnp
from jax import lax
from jax.sharding import PartitionSpec as P


def count_product(rows, codes, offset, row_scale):
    seed_count, fanout = codes.shape
    block_size = math.gcd(seed_count, 128)
    row_count = rows.shape[0]
    code_iota = lax.broadcasted_iota(jnp.int32, (1, row_count), 1) + offset

    def per_block(block_codes):
        tally = jnp.zeros((block_size, row_count), jnp.float32)
        for column in range(fanout):
            tally = tally + (block_codes[:, column : column + 1] == code_iota).astype(jnp.float32)
        tally = tally * row_scale[None, :]
        return jnp.dot(
            tally, rows, precision=lax.Precision.HIGHEST, preferred_element_type=jnp.float32
        )

    summed = lax.map(per_block, codes.reshape(-1, block_size, fanout))
    return summed.reshape(seed_count, rows.shape[1])


def project(values, weight):
    return jnp.dot(
        values, weight, precision=lax.Precision.HIGHEST, preferred_element_type=jnp.float32
    )


def local(features, seed_self, hub_ids, requests, counts, neighbors, weight, out_bias):
    shard_count = lax.axis_size("shard")
    capacity = requests.shape[1]
    feat_width = features.shape[1]
    hub_total = hub_ids.shape[0] * lax.axis_size("rep")
    local_hubs = jnp.take(features, hub_ids, axis=0)
    slot_index = lax.broadcasted_iota(jnp.int32, (shard_count, capacity), 1)
    slot_live = (slot_index < counts[:, None]).astype(jnp.float32).reshape(-1)
    code_live = jnp.concatenate([jnp.ones((hub_total,), jnp.float32), slot_live])
    weights = jnp.take(code_live, neighbors)
    taken = 1.0 + jnp.sum(weights, axis=1)
    hub_rows = lax.all_gather(local_hubs, "rep", axis=0, tiled=True)
    hub_part = count_product(hub_rows, neighbors, 0, jnp.ones((hub_total,), jnp.float32))
    looked = jnp.take(
        features, lax.all_to_all(requests, "shard", split_axis=0, concat_axis=0, tiled=True), axis=0
    )
    fetched = lax.all_to_all(looked, "shard", split_axis=0, concat_axis=0, tiled=True)
    slot_rows = fetched.reshape(-1, feat_width)
    slot_part = count_product(slot_rows, neighbors, hub_total, slot_live)
    total = seed_self + (hub_part + slot_part)
    mean_rows = total / taken[:, None]
    product = project(mean_rows, weight)
    return jnp.maximum(product + out_bias, 0.0)


def solution(mesh):
    return jax.shard_map(
        local,
        mesh=mesh,
        in_specs=(
            P(("rep", "shard"), None),
            P(("rep", "shard"), None),
            P(("rep", "shard")),
            P(("rep", "shard"), None),
            P(("rep", "shard")),
            P(("rep", "shard"), None),
            P(),
            P(),
        ),
        out_specs=P(("rep", "shard"), None),
        check_vma=False,
    )
```

profile of v0, /device:TPU:0, one launch (start us, length us, event | category | flops | bytes accessed | tf_op | source)
XLA Modules:
  0.0 37.0 jit_solution(1455155119561866945)
XLA Ops:
  0.0 0.0 copy-start
  0.0 0.0 copy-start.6
  0.0 7.5 %all-to-all-start = ((s32[16,1,32]{2,1,0:T(1,128)}), s32[16,1,32]{2,1,0:T(1,128)S(1)}, u32[]{:S(2)}, u32[]{:S(2)}) async-start(s32[16,1,32]{2,1,0:T(1,128)} %bitcast.45), calls=%async_computation | async-start | bytes 16384 | tf_op jit(solution)/shard_map/all_to_all | solution.py:48
  7.6 0.0 copy-done.6
  7.6 0.0 copy-start.2
  7.6 0.6 %copy-done.2 = s32[128,15]{0,1:T(8,128)S(1)} copy-done((s32[128,15]{0,1:T(8,128)S(1)}, s32[128,15]{0,1:T(8,128)}, u32[]{:S(2)}) %copy-start.2) | copy-done | bytes 7704
  8.3 0.0 copy-done
  8.3 0.8 %gather_fusion = f32[128,256]{1,0:T(8,128)S(1)} fusion(f32[512,256]{1,0:T(8,128)S(1)} %copy-done, s32[1024]{0:T(1024)S(1)} %pad_clamp_fusion.2), kind=kCustom, calls=%fused_computation | custom fusion | bytes 262656 | tf_op jit(solution)/shard_map/jit(_take)/gather | solution.py:39
  9.0 0.0 copy-start.4
  9.0 0.1 broadcast_select_fusion.1
  9.1 0.6 %copy-done.4 = s32[16]{0:T(128)S(1)} copy-done((s32[16]{0:T(128)S(1)}, s32[16]{0:T(128)}, u32[]{:S(2)}) %copy-start.4) | copy-done | bytes 88
  9.7 0.1 fusion.110
  9.8 0.1 copy.19
  9.9 0.2 reshape.107
  10.1 3.8 %all-to-all-done = s32[16,1,32]{2,1,0:T(1,128)S(1)} async-done(((s32[16,1,32]{2,1,0:T(1,128)}), s32[16,1,32]{2,1,0:T(1,128)S(1)}, u32[]{:S(2)}, u32[]{:S(2)}) %all-to-all-start) | async-done | bytes 2080 | tf_op jit(solution)/shard_map/all_to_all | solution.py:48
  13.9 0.1 reshape.99
  14.0 1.6 %gather_fusion.1 = f32[512,256]{1,0:T(8,128)S(1)} fusion(f32[512,256]{1,0:T(8,128)S(1)} %copy-done, s32[1024]{0:T(1024)S(1)} %pad_clamp_fusion.1), kind=kCustom, calls=%fused_computation.1 | custom fusion | bytes 1050624 | tf_op jit(solution)/shard_map/jit(_take)/gather | solution.py:47
  15.6 0.9 %broadcast_select_fusion = f32[16,32,256]{2,1,0:T(8,128)} fusion(f32[16,32,256]{2,1,0:T(8,128)S(1)} %bitcast.41, pred[16,32]{1,0:T(8,128)(4,1)S(1)} %compare_and_fusion), kind=kLoop, calls=%fused_computation.8 | loop fusion | flops 131072 | bytes 1049088 | tf_op jit(solution)/shard_map/jit(_take)/select_n | solution.py:47
  16.5 3.6 %all-to-all-start.1 = ((f32[16,32,256]{2,1,0:T(8,128)}), f32[16,32,256]{2,1,0:T(8,128)S(1)}, u32[]{:S(2)}, u32[]{:S(2)}) async-start(f32[16,32,256]{2,1,0:T(8,128)} %broadcast_select_fusion), calls=%async_computation.1 | async-start | bytes 1048576 | tf_op jit(solution)/shard_map/all_to_all | solution.py:50
  20.1 0.1 reshape.88
  20.2 7.2 %gather_fusion.2 = f32[1920]{0:T(1024)S(1)} fusion(f32[768]{0:T(1024)S(1)} %concatenate.3, s32[2048]{0:T(1024)S(1)} %pad_clamp_fusion), kind=kCustom, calls=%fused_computation.2 | custom fusion | bytes 23040 | tf_op jit(solution)/shard_map/jit(_take)/gather | solution.py:43
  27.4 0.2 reshape.106
  27.6 0.1 copy.20
  27.7 6.4 %all_gather.3 = f32[256,256]{1,0:T(8,128)S(1)} all-gather(f32[128,256]{1,0:T(8,128)S(1)} %broadcast_select_fusion.1), channel_id=1, replica_groups=mesh['rep'=2,'shard'=16] {'rep'}, dimensions={0}, use_global_device_ids=true | all-gather | bytes 393216 | tf_op jit(solution)/shard_map/all_gather | solution.py:45
  34.1 0.0 copy-start.5
  34.1 0.9 %fusion.50 = f32[128,256]{1,0:T(8,128)S(1)} fusion(f32[256,256]{1,0:T(8,128)S(1)} %all_gather.3, s32[128]{0:T(128)S(1)} %get-tuple-element.52, s32[128]{0:T(128)S(1)} %get-tuple-element.25, s32[128]{0:T(128)S(1)} %get-tuple-element.32, s32[128]{0:T(128)S(1)} %get-tuple-element.33, s32[128]{0:T(128)S(1)} %get-tuple-element.34, ...), kind=kOutput, calls=%fused_computation.56 | convolution fusion | flops 102105088 | bytes 400896 | tf_op jit(solution)/shard_map/while/body/eval_jaxpr/dot_general | solution.py:20
  35.0 0.0 all-to-all-done.1
  35.0 0.0 copy-done.5
  35.1 0.0 copy-start.1
  35.1 0.0 copy-start.3
  35.1 0.9 %fusion.2 = f32[128,256]{1,0:T(8,128)S(1)} fusion(f32[128,256]{1,0:T(8,128)S(1)} %copy-done.5, f32[128,256]{1,0:T(8,128)S(1)} %fusion.50, f32[512,256]{1,0:T(8,128)S(1)} %bitcast.42, f32[512]{0:T(512)S(1)} %reshape.88, s32[512]{0:T(512)S(1)} %iota_add_fusion, s32[128]{0:T(128)S(1)} %get-tuple-element.52, s32[128]{0:T(128)S(1)} %get-tuple-element.25, ...), kind=kOutput, calls=%fused_computation.7 | convolution fusion | flops 204374016 | bytes 929792 | tf_op jit(solution)/shard_map/while/body/eval_jaxpr/dot_general | solution.py:20
  35.9 0.1 copy-done.1
  36.0 0.0 copy-done.3
  36.0 0.9 %fusion = f32[128,256]{1,0:T(8,128)} fusion(f32[128,256]{1,0:T(8,128)S(1)} %fusion.2, f32[256,256]{1,0:T(8,128)S(1)} %copy-done.1, f32[256]{0:T(256)S(1)} %copy-done.3), kind=kOutput, calls=%fused_computation.4 | convolution fusion | flops 100728832 | bytes 525312 | tf_op jit(solution)/shard_map/dot_general | solution.py:29
  (13 shorter events, 0.1 us)
Async XLA Ops:
  0.0 8.3 %copy-start = (f32[512,256]{1,0:T(8,128)S(1)}, f32[512,256]{1,0:T(8,128)}, u32[]{:S(2)}) copy-start(f32[512,256]{1,0:T(8,128)} %param.8) | copy-start | bytes 1572868
  0.0 7.6 %copy-start.6 = (s32[128]{0:T(128)S(1)}, s32[128]{0:T(128)}, u32[]{:S(2)}) copy-start(s32[128]{0:T(128)} %param.10) | copy-start | bytes 1540
  0.0 13.9 %all-to-all-start = ((s32[16,1,32]{2,1,0:T(1,128)}), s32[16,1,32]{2,1,0:T(1,128)S(1)}, u32[]{:S(2)}, u32[]{:S(2)}) async-start(s32[16,1,32]{2,1,0:T(1,128)} %bitcast.45), calls=%async_computation | async-start | bytes 16384 | tf_op jit(solution)/shard_map/all_to_all | solution.py:48
  7.6 0.7 %copy-start.2 = (s32[128,15]{0,1:T(8,128)S(1)}, s32[128,15]{0,1:T(8,128)}, u32[]{:S(2)}) copy-start(s32[128,15]{0,1:T(8,128)} %param.13) | copy-start | bytes 23044
  9.0 0.7 %copy-start.4 = (s32[16]{0:T(128)S(1)}, s32[16]{0:T(128)}, u32[]{:S(2)}) copy-start(s32[16]{0:T(128)} %param.12) | copy-start | bytes 196
  16.5 18.5 %all-to-all-start.1 = ((f32[16,32,256]{2,1,0:T(8,128)}), f32[16,32,256]{2,1,0:T(8,128)S(1)}, u32[]{:S(2)}, u32[]{:S(2)}) async-start(f32[16,32,256]{2,1,0:T(8,128)} %broadcast_select_fusion), calls=%async_computation.1 | async-start | bytes 1048576 | tf_op jit(solution)/shard_map/all_to_all | solution.py:50
  34.1 0.9 %copy-start.5 = (f32[128,256]{1,0:T(8,128)S(1)}, f32[128,256]{1,0:T(8,128)}, u32[]{:S(2)}) copy-start(f32[128,256]{1,0:T(8,128)} %param.9) | copy-start | bytes 393220
  35.1 1.0 %copy-start.1 = (f32[256,256]{1,0:T(8,128)S(1)}, f32[256,256]{1,0:T(8,128)}, u32[]{:S(2)}) copy-start(f32[256,256]{1,0:T(8,128)} %param.14) | copy-start | bytes 786436
  35.1 0.9 %copy-start.3 = (f32[256]{0:T(256)S(1)}, f32[256]{0:T(256)}, u32[]{:S(2)}) copy-start(f32[256]{0:T(256)} %param.15) | copy-start | bytes 3076
where the time goes:
time: 37.3 us; the launch traced here: 37 us
  local copies, waits for them, and re-layouts  11.6 us (31%)
  starting transfers between devices  11.1 us (30%)
  blocking collectives  6.37 us (17%)
  waiting for transfers between devices  3.84 us (10%)
  matrix products  2.69 us (7%)
  other arithmetic  1.17 us (3%)
    all_to_all x1, starting transfers between devices, local(): lax.all_to_all(requests, 'shard', split_axis=0, concat_axis=0, tiled=True)  7.55 us
    gather x3, local copies, waits for them, and re-layouts, local(): weights = jnp.take(code_live, neighbors)  7.47 us
    all_gather x1, blocking collectives, local(): hub_rows = lax.all_gather(local_hubs, 'rep', axis=0, tiled=True)  6.37 us
    all_to_all x1, waiting for transfers between devices, local(): lax.all_to_all(requests, 'shard', split_axis=0, concat_axis=0, tiled=True)  3.84 us
    all_to_all x1, starting transfers between devices, local(): lax.all_to_all(looked, 'shard', split_axis=0, concat_axis=0, tiled=True)  3.57 us
    dot_general x2, matrix products, per_block(): jnp.dot(tally, rows, precision=lax.Precision.HIGHEST, preferred_element_t...  1.75 us
    gather x1, local copies, waits for them, and re-layouts, local(): jnp.take(features, lax.all_to_all(requests, 'shard', split_axis=0, concat...  1.57 us
    unnamed x14, local copies, waits for them, and re-layouts  1.31 us
  transfers between devices with their start and end apart: 2, of which 1 were waited for; matrix products, arithmetic and copies ran while one was open for 26% of the time, Pallas kernels for 0%

commit v1 on v0

v1 whole, which is shorter than its diff:
```python
import jax
import jax.numpy as jnp
from jax import lax
from jax.sharding import PartitionSpec as P


def dot(a, b):
    return jnp.dot(a, b, precision=lax.Precision.HIGH, preferred_element_type=jnp.float32)


def tally_of(codes, code_row):
    tally = jnp.zeros((codes.shape[0], code_row.shape[1]), jnp.float32)
    for column in range(codes.shape[1]):
        tally = tally + (codes[:, column : column + 1] == code_row).astype(jnp.float32)
    return tally


def local(features, seed_self, hub_ids, requests, counts, neighbors, weight, out_bias):
    shard_count, capacity = requests.shape
    feat_width = features.shape[1]
    reps = lax.axis_size("rep")
    rep = lax.axis_index("rep")
    hubs = hub_ids.shape[0]
    hub_total = hubs * reps

    asked = lax.all_to_all(requests, "shard", split_axis=0, concat_axis=0, tiled=True)

    own = features.at[hub_ids].get(mode="promise_in_bounds")
    blocks = [own]
    offsets = [rep * hubs]
    for k in range(1, reps):
        blocks.append(lax.ppermute(own, "rep", [(i, (i + k) % reps) for i in range(reps)]))
        offsets.append(((rep - k) % reps) * hubs)
    hub_iota = lax.broadcasted_iota(jnp.int32, (1, hubs), 1)
    hub_codes = jnp.concatenate([hub_iota + o for o in offsets], axis=1)

    slot = lax.broadcasted_iota(jnp.int32, (shard_count, capacity), 1)
    flat = lax.broadcasted_iota(jnp.int32, (shard_count, capacity), 0) * capacity + slot
    slot_codes = jnp.where(slot < counts[:, None], flat + hub_total, -1).reshape(1, -1)
    hub_tally = tally_of(neighbors, hub_codes)
    slot_tally = tally_of(neighbors, slot_codes)
    taken = 1.0 + jnp.sum(hub_tally, axis=1) + jnp.sum(slot_tally, axis=1)
    hub_tally, slot_tally, taken, asked = lax.optimization_barrier(
        (hub_tally, slot_tally, taken, asked)
    )

    looked = features.at[asked].get(mode="promise_in_bounds")
    fetched = lax.all_to_all(looked, "shard", split_axis=0, concat_axis=0, tiled=True)
    hub_rows = jnp.concatenate(blocks, axis=0)
    base = seed_self + dot(hub_tally, hub_rows)
    total = base + dot(slot_tally, fetched.reshape(-1, feat_width))
    mean_rows = total / taken[:, None]
    return jnp.maximum(dot(mean_rows, weight) + out_bias, 0.0)


def solution(mesh):
    both = P(("rep", "shard"))
    return jax.shard_map(
        local,
        mesh=mesh,
        in_specs=(both, both, both, both, both, both, P(), P()),
        out_specs=both,
        check_vma=False,
    )
```

time: 37.3 us -> 36.7 us (0.984)
  waiting for transfers between devices: 3.84 us -> 15.7 us
  local copies, waits for them, and re-layouts: 11.6 us -> 5.19 us
  blocking collectives: 6.37 us -> 0 us
  starting transfers between devices: 11.1 us -> 12.8 us
  matrix products: 2.69 us -> 1.41 us
    all_to_all x1, waiting for transfers between devices: 0.01 us -> 11.9 us  [local(): lax.all_to_all(looked, 'shard', split_axis=0, concat_axis=0, tiled=True)]
    gather x5 -> x2, local copies, waits for them, and re-layouts: 9.79 us -> 2.99 us  [the longest x1 2.24 us: local(): looked = features.at[asked].get(mode='promise_in_bounds')]
    all_gather x1 -> x0, blocking collectives: 6.37 us -> none  [local(): hub_rows = lax.all_gather(local_hubs, 'rep', axis=0, tiled=True)]
    ppermute x0 -> x1, starting transfers between devices: none -> 1.56 us  [local(): lax.ppermute(own, 'rep', [(i, (i + k) % reps) for i in range(reps)])]
    dot_general x3, matrix products: 2.69 us -> 1.41 us  [dot(): jnp.dot(a, b, precision=lax.Precision.HIGH, preferred_element_type=jnp.fl...]
    select_n x5 -> x3, other arithmetic: 1.03 us -> 0.08 us  [the longest x1 0.07 us: local(): jnp.where(slot < counts[:, None], flat + hub_total, -1).reshape(1, -1)]
    reduce_sum x1 -> x2, other arithmetic: 0.02 us -> 0.95 us  [local(): taken = 1.0 + jnp.sum(hub_tally, axis=1) + jnp.sum(slot_tally, axis=1)]
    unnamed x14, local copies, waits for them, and re-layouts: 1.31 us -> 2.03 us
  transfers between devices with their start and end apart: 2 -> 3, of which waited for: 1 -> 2; matrix products, arithmetic and copies ran while one was open for 26% -> 6% of each run, Pallas kernels for 0% -> 0%
where the time goes in v1:
time: 36.7 us; the launch traced here: 36.4 us
  waiting for transfers between devices  15.7 us (43%)
  starting transfers between devices  12.8 us (35%)
  local copies, waits for them, and re-layouts  5.19 us (14%)
  matrix products  1.41 us (4%)
  other arithmetic  1.07 us (3%)
    all_to_all x1, waiting for transfers between devices, local(): lax.all_to_all(looked, 'shard', split_axis=0, concat_axis=0, tiled=True)  11.9 us
    all_to_all x1, starting transfers between devices, local(): lax.all_to_all(requests, 'shard', split_axis=0, concat_axis=0, tiled=True)  7.55 us
    all_to_all x1, waiting for transfers between devices, local(): lax.all_to_all(requests, 'shard', split_axis=0, concat_axis=0, tiled=True)  3.86 us
    all_to_all x1, starting transfers between devices, local(): lax.all_to_all(looked, 'shard', split_axis=0, concat_axis=0, tiled=True)  3.7 us
    gather x1, local copies, waits for them, and re-layouts, local(): looked = features.at[asked].get(mode='promise_in_bounds')  2.24 us
    unnamed x14, local copies, waits for them, and re-layouts  2.03 us
    ppermute x1, starting transfers between devices, local(): lax.ppermute(own, 'rep', [(i, (i + k) % reps) for i in range(reps)])  1.56 us
    dot_general x3, matrix products, dot(): jnp.dot(a, b, precision=lax.Precision.HIGH, preferred_element_type=jnp.fl...  1.41 us
  transfers between devices with their start and end apart: 3, of which 2 were waited for; matrix products, arithmetic and copies ran while one was open for 6% of the time, Pallas kernels for 0%

profile of v1, /device:TPU:0, one launch (start us, length us, event | category | flops | bytes accessed | tf_op | source)
XLA Modules:
  0.0 36.4 jit_solution(10898484274152713867)
XLA Ops:
  0.0 0.0 copy-start
  0.0 7.5 %all-to-all-start = ((s32[16,1,32]{2,1,0:T(1,128)}), s32[16,1,32]{2,1,0:T(1,128)S(1)}, u32[]{:S(2)}, u32[]{:S(2)}) async-start(s32[16,1,32]{2,1,0:T(1,128)} %bitcast.42), calls=%async_computation | async-start | bytes 16384 | tf_op jit(solution)/shard_map/all_to_all | solution.py:26
  7.6 0.0 copy-start.3
  7.6 0.7 %copy-done.3 = s32[128,15]{0,1:T(8,128)S(1)} copy-done((s32[128,15]{0,1:T(8,128)S(1)}, s32[128,15]{0,1:T(8,128)}, u32[]{:S(2)}) %copy-start.3) | copy-done | bytes 7704
  8.3 0.0 copy-start.5
  8.3 0.6 %copy-done.5 = s32[16]{0:T(128)S(1)} copy-done((s32[16]{0:T(128)S(1)}, s32[16]{0:T(128)}, u32[]{:S(2)}) %copy-start.5) | copy-done | bytes 88
  8.9 0.1 add_select_fusion
  9.0 0.1 select_n.26
  9.1 0.5 %fusion.8 = (f32[128]{0:T(128)S(1)}, f32[128,512]{1,0:T(8,128)S(1)}) fusion(s32[128]{0:T(128)S(1)} %get-tuple-element.30, s32[128]{0:T(128)S(1)} %get-tuple-element.31, s32[128]{0:T(128)S(1)} %get-tuple-element.18, s32[128]{0:T(128)S(1)} %get-tuple-element.19, s32[128]{0:T(128)S(1)} %get-tuple-element.20, s32[128]{0:T(128)S(1)} %get-tuple-element.21, ...), kind=kLoop, calls=%fused_computation.40 | loop fusion | flops 2948992 | bytes 272384 | tf_op jit(solution)/shard_map/reduce_sum | solution.py:42
  9.6 0.4 %fusion.7 = (f32[128]{0:T(128)S(1)}, f32[128,256]{1,0:T(8,128)S(1)}) fusion(s32[128]{0:T(128)S(1)} %get-tuple-element.30, s32[128]{0:T(128)S(1)} %get-tuple-element.31, s32[128]{0:T(128)S(1)} %get-tuple-element.18, s32[128]{0:T(128)S(1)} %get-tuple-element.19, s32[128]{0:T(128)S(1)} %get-tuple-element.20, s32[128]{0:T(128)S(1)} %get-tuple-element.21, ...), kind=kLoop, calls=%fused_computation.39 | loop fusion | flops 1474432 | bytes 140288 | tf_op jit(solution)/shard_map/reduce_sum | solution.py:42
  10.1 3.9 %all-to-all-done = s32[16,1,32]{2,1,0:T(1,128)S(1)} async-done(((s32[16,1,32]{2,1,0:T(1,128)}), s32[16,1,32]{2,1,0:T(1,128)S(1)}, u32[]{:S(2)}, u32[]{:S(2)}) %all-to-all-start) | async-done | bytes 2080 | tf_op jit(solution)/shard_map/all_to_all | solution.py:26
  13.9 0.1 reshape.70
  14.0 0.0 copy-done
  14.0 2.2 %gather_fusion.1 = f32[512,256]{1,0:T(8,128)} fusion(f32[512,256]{1,0:T(8,128)S(1)} %copy-done, s32[1024]{0:T(1024)S(1)} %pad_clamp_fusion), kind=kCustom, calls=%fused_computation.1 | custom fusion | bytes 1050624 | tf_op jit(solution)/shard_map/gather | solution.py:47
  16.3 0.0 copy-start.6
  16.3 3.7 %all-to-all-start.1 = ((f32[16,32,256]{2,1,0:T(8,128)}), f32[16,32,256]{2,1,0:T(8,128)S(1)}, u32[]{:S(2)}, u32[]{:S(2)}) async-start(f32[16,32,256]{2,1,0:T(8,128)} %bitcast.18), calls=%async_computation.1 | async-start | bytes 1048576 | tf_op jit(solution)/shard_map/all_to_all | solution.py:48
  20.0 0.0 copy-done.6
  20.0 0.8 %gather_fusion = f32[128,256]{1,0:T(8,128)S(1)} fusion(f32[512,256]{1,0:T(8,128)S(1)} %copy-done, s32[1024]{0:T(1024)S(1)} %pad_clamp_fusion.1), kind=kCustom, calls=%fused_computation | custom fusion | bytes 262656 | tf_op jit(solution)/shard_map/gather | solution.py:28
  20.8 1.6 %collective-permute-start = (f32[128,256]{1,0:T(8,128)S(1)}, f32[128,256]{1,0:T(8,128)S(1)}, u32[]{:S(2)}, u32[]{:S(2)}) collective-permute-start(f32[128,256]{1,0:T(8,128)S(1)} %gather_fusion), channel_id=1, source_target_pairs={{0,16},{16,0},{1,17},{17,1},{2,18},{18,2},{3,19},{19,3},{4,20},{20... | collective-permute-start | bytes 393224 | tf_op jit(solution)/shard_map/ppermute | solution.py:32
  22.3 11.9 %all-to-all-done.1 = f32[16,32,256]{2,1,0:T(8,128)S(1)} async-done(((f32[16,32,256]{2,1,0:T(8,128)}), f32[16,32,256]{2,1,0:T(8,128)S(1)}, u32[]{:S(2)}, u32[]{:S(2)}) %all-to-all-start.1) | async-done | bytes 524320 | tf_op jit(solution)/shard_map/all_to_all | solution.py:48
  34.2 0.0 copy-start.2
  34.2 0.3 fusion.9
  34.5 0.0 copy-start.1
  34.5 0.0 copy-start.4
  34.5 0.0 collective-permute-done
  34.5 0.6 %copy-done.2 = f32[128,256]{1,0:T(8,128)S(1)} copy-done((f32[128,256]{1,0:T(8,128)S(1)}, f32[128,256]{1,0:T(8,128)}, u32[]{:S(2)}) %copy-start.2) | copy-done | bytes 131096
  35.1 0.2 fusion.2
  35.4 0.1 copy-done.1
  35.5 0.0 copy-done.4
  35.5 0.9 %fusion = f32[128,256]{1,0:T(8,128)} fusion(f32[128,256]{1,0:T(8,128)S(1)} %fusion.2, f32[256,256]{1,0:T(8,128)S(1)} %copy-done.1, f32[256]{0:T(256)S(1)} %copy-done.4), kind=kOutput, calls=%fused_computation.3 | convolution fusion | flops 50397184 | bytes 525312 | tf_op jit(solution)/shard_map/dot_general | solution.py:8
  (9 shorter events, 0.0 us)
Async XLA Ops:
  0.0 14.0 %copy-start = (f32[512,256]{1,0:T(8,128)S(1)}, f32[512,256]{1,0:T(8,128)}, u32[]{:S(2)}) copy-start(f32[512,256]{1,0:T(8,128)} %param.8) | copy-start | bytes 1572868
  0.0 13.9 %all-to-all-start = ((s32[16,1,32]{2,1,0:T(1,128)}), s32[16,1,32]{2,1,0:T(1,128)S(1)}, u32[]{:S(2)}, u32[]{:S(2)}) async-start(s32[16,1,32]{2,1,0:T(1,128)} %bitcast.42), calls=%async_computation | async-start | bytes 16384 | tf_op jit(solution)/shard_map/all_to_all | solution.py:26
  7.6 0.7 %copy-start.3 = (s32[128,15]{0,1:T(8,128)S(1)}, s32[128,15]{0,1:T(8,128)}, u32[]{:S(2)}) copy-start(s32[128,15]{0,1:T(8,128)} %param.13) | copy-start | bytes 23044
  8.3 0.7 %copy-start.5 = (s32[16]{0:T(128)S(1)}, s32[16]{0:T(128)}, u32[]{:S(2)}) copy-start(s32[16]{0:T(128)} %param.12) | copy-start | bytes 196
  16.3 3.7 %copy-start.6 = (s32[128]{0:T(128)S(1)}, s32[128]{0:T(128)}, u32[]{:S(2)}) copy-start(s32[128]{0:T(128)} %param.10) | copy-start | bytes 1540
  16.3 17.9 %all-to-all-start.1 = ((f32[16,32,256]{2,1,0:T(8,128)}), f32[16,32,256]{2,1,0:T(8,128)S(1)}, u32[]{:S(2)}, u32[]{:S(2)}) async-start(f32[16,32,256]{2,1,0:T(8,128)} %bitcast.18), calls=%async_computation.1 | async-start | bytes 1048576 | tf_op jit(solution)/shard_map/all_to_all | solution.py:48
  20.8 13.8 %collective-permute-start = (f32[128,256]{1,0:T(8,128)S(1)}, f32[128,256]{1,0:T(8,128)S(1)}, u32[]{:S(2)}, u32[]{:S(2)}) collective-permute-start(f32[128,256]{1,0:T(8,128)S(1)} %gather_fusion), channel_id=1, source_target_pairs={{0,16},{16,0},{1,17},{17,1},{2,18},{18,2},{3,19},{19,3},{4,20},{20... | collective-permute-start | bytes 393224 | tf_op jit(solution)/shard_map/ppermute | solution.py:32
  34.2 0.9 %copy-start.2 = (f32[128,256]{1,0:T(8,128)S(1)}, f32[128,256]{1,0:T(8,128)}, u32[]{:S(2)}) copy-start(f32[128,256]{1,0:T(8,128)} %param.9) | copy-start | bytes 393220
  34.5 1.0 %copy-start.1 = (f32[256,256]{1,0:T(8,128)S(1)}, f32[256,256]{1,0:T(8,128)}, u32[]{:S(2)}) copy-start(f32[256,256]{1,0:T(8,128)} %param.14) | copy-start | bytes 786436
  34.5 1.0 %copy-start.4 = (f32[256]{0:T(256)S(1)}, f32[256]{0:T(256)}, u32[]{:S(2)}) copy-start(f32[256]{0:T(256)} %param.15) | copy-start | bytes 3076

commit v2 on v1

--- a/solution.py
+++ b/solution.py
@@ -44,7 +44,15 @@
         (hub_tally, slot_tally, taken, asked)
     )
 
-    looked = features.at[asked].get(mode="promise_in_bounds")
+    row_iota = lax.broadcasted_iota(jnp.int32, (1, 1, features.shape[0]), 2)
+    picks = (asked[:, :, None] == row_iota).astype(jnp.float32)
+    looked = lax.dot_general(
+        picks,
+        features,
+        (((2,), (0,)), ((), ())),
+        precision=lax.Precision.HIGH,
+        preferred_element_type=jnp.float32,
+    )
     fetched = lax.all_to_all(looked, "shard", split_axis=0, concat_axis=0, tiled=True)
     hub_rows = jnp.concatenate(blocks, axis=0)
     base = seed_self + dot(hub_tally, hub_rows)

time: 36.7 us -> 35.7 us (0.973)
  local copies, waits for them, and re-layouts: 5.19 us -> 2.88 us
  matrix products: 1.41 us -> 2.69 us
    gather x1 -> x0, local copies, waits for them, and re-layouts: 2.24 us -> none  [local(): looked = features.at[asked].get(mode='promise_in_bounds')]
    dot_general x0 -> x1, matrix products: none -> 1.28 us  [local(): lax.dot_general(picks, features, (((2,), (0,)), ((), ())), precision=lax....]
where the time goes in v2:
time: 35.7 us; the launch traced here: 35.3 us
  waiting for transfers between devices  15.7 us (44%)
  starting transfers between devices  12.8 us (36%)
  local copies, waits for them, and re-layouts  2.88 us (8%)
  matrix products  2.69 us (8%)
  other arithmetic  1.06 us (3%)
    all_to_all x1, waiting for transfers between devices, local(): lax.all_to_all(looked, 'shard', split_axis=0, concat_axis=0, tiled=True)  11.9 us
    all_to_all x1, starting transfers between devices, local(): lax.all_to_all(requests, 'shard', split_axis=0, concat_axis=0, tiled=True)  7.55 us
    all_to_all x1, waiting for transfers between devices, local(): lax.all_to_all(requests, 'shard', split_axis=0, concat_axis=0, tiled=True)  3.85 us
    all_to_all x1, starting transfers between devices, local(): lax.all_to_all(looked, 'shard', split_axis=0, concat_axis=0, tiled=True)  3.7 us
    unnamed x14, local copies, waits for them, and re-layouts  2.04 us
    ppermute x1, starting transfers between devices, local(): lax.ppermute(own, 'rep', [(i, (i + k) % reps) for i in range(reps)])  1.56 us
    dot_general x3, matrix products, dot(): jnp.dot(a, b, precision=lax.Precision.HIGH, preferred_element_type=jnp.fl...  1.41 us
    dot_general x1, matrix products, local(): lax.dot_general(picks, features, (((2,), (0,)), ((), ())), precision=lax....  1.28 us
  transfers between devices with their start and end apart: 3, of which 2 were waited for; matrix products, arithmetic and copies ran while one was open for 6% of the time, Pallas kernels for 0%

profile of v2, /device:TPU:0, one launch (start us, length us, event | category | flops | bytes accessed | tf_op | source)
XLA Modules:
  0.0 35.3 jit_solution(3435506387590132599)
XLA Ops:
  0.0 0.0 copy-start
  0.0 7.5 %all-to-all-start = ((s32[16,1,32]{2,1,0:T(1,128)}), s32[16,1,32]{2,1,0:T(1,128)S(1)}, u32[]{:S(2)}, u32[]{:S(2)}) async-start(s32[16,1,32]{2,1,0:T(1,128)} %bitcast.44), calls=%async_computation | async-start | bytes 16384 | tf_op jit(solution)/shard_map/all_to_all | solution.py:26
  7.6 0.0 copy-start.3
  7.6 0.7 %copy-done.3 = s32[128,15]{0,1:T(8,128)S(1)} copy-done((s32[128,15]{0,1:T(8,128)S(1)}, s32[128,15]{0,1:T(8,128)}, u32[]{:S(2)}) %copy-start.3) | copy-done | bytes 7704
  8.3 0.0 copy-start.5
  8.3 0.6 %copy-done.5 = s32[16]{0:T(128)S(1)} copy-done((s32[16]{0:T(128)S(1)}, s32[16]{0:T(128)}, u32[]{:S(2)}) %copy-start.5) | copy-done | bytes 88
  8.9 0.1 add_select_fusion
  9.0 0.1 select_n.23
  9.1 0.5 %fusion.11 = (f32[128]{0:T(128)S(1)}, f32[128,512]{1,0:T(8,128)S(1)}) fusion(s32[128]{0:T(128)S(1)} %get-tuple-element.30, s32[128]{0:T(128)S(1)} %get-tuple-element.31, s32[128]{0:T(128)S(1)} %get-tuple-element.18, s32[128]{0:T(128)S(1)} %get-tuple-element.19, s32[128]{0:T(128)S(1)} %get-tuple-element.20, s32[128]{0:T(128)S(1)} %get-tuple-element.21, ...), kind=kLoop, calls=%fused_computation.41 | loop fusion | flops 2948992 | bytes 272384 | tf_op jit(solution)/shard_map/reduce_sum | solution.py:42
  9.6 0.4 %fusion.10 = (f32[128]{0:T(128)S(1)}, f32[128,256]{1,0:T(8,128)S(1)}) fusion(s32[128]{0:T(128)S(1)} %get-tuple-element.30, s32[128]{0:T(128)S(1)} %get-tuple-element.31, s32[128]{0:T(128)S(1)} %get-tuple-element.18, s32[128]{0:T(128)S(1)} %get-tuple-element.19, s32[128]{0:T(128)S(1)} %get-tuple-element.20, s32[128]{0:T(128)S(1)} %get-tuple-element.21, ...), kind=kLoop, calls=%fused_computation.40 | loop fusion | flops 1474432 | bytes 140288 | tf_op jit(solution)/shard_map/reduce_sum | solution.py:42
  10.1 3.9 %all-to-all-done = s32[16,1,32]{2,1,0:T(1,128)S(1)} async-done(((s32[16,1,32]{2,1,0:T(1,128)}), s32[16,1,32]{2,1,0:T(1,128)S(1)}, u32[]{:S(2)}, u32[]{:S(2)}) %all-to-all-start) | async-done | bytes 2080 | tf_op jit(solution)/shard_map/all_to_all | solution.py:26
  13.9 0.0 copy-done
  13.9 1.3 %fusion.3 = f32[16,32,256]{2,1,0:T(8,128)} fusion(f32[512,256]{1,0:T(8,128)S(1)} %copy-done, s32[16,32]{1,0:T(8,128)S(1)} %bitcast.43), kind=kOutput, calls=%fused_computation.7 | convolution fusion | flops 402915328 | bytes 1050624 | tf_op jit(solution)/shard_map/dot_general | solution.py:49
  15.2 0.0 copy-start.6
  15.2 3.7 %all-to-all-start.1 = ((f32[16,32,256]{2,1,0:T(8,128)}), f32[16,32,256]{2,1,0:T(8,128)S(1)}, u32[]{:S(2)}, u32[]{:S(2)}) async-start(f32[16,32,256]{2,1,0:T(8,128)} %fusion.3), calls=%async_computation.1 | async-start | bytes 1048576 | tf_op jit(solution)/shard_map/all_to_all | solution.py:56
  18.9 0.0 copy-done.6
  19.0 0.8 %gather_fusion = f32[128,256]{1,0:T(8,128)S(1)} fusion(f32[512,256]{1,0:T(8,128)S(1)} %copy-done, s32[1024]{0:T(1024)S(1)} %pad_clamp_fusion), kind=kCustom, calls=%fused_computation | custom fusion | bytes 262656 | tf_op jit(solution)/shard_map/gather | solution.py:28
  19.7 1.6 %collective-permute-start = (f32[128,256]{1,0:T(8,128)S(1)}, f32[128,256]{1,0:T(8,128)S(1)}, u32[]{:S(2)}, u32[]{:S(2)}) collective-permute-start(f32[128,256]{1,0:T(8,128)S(1)} %gather_fusion), channel_id=1, source_target_pairs={{0,16},{16,0},{1,17},{17,1},{2,18},{18,2},{3,19},{19,3},{4,20},{20... | collective-permute-start | bytes 393224 | tf_op jit(solution)/shard_map/ppermute | solution.py:32
  21.3 11.9 %all-to-all-done.1 = f32[16,32,256]{2,1,0:T(8,128)S(1)} async-done(((f32[16,32,256]{2,1,0:T(8,128)}), f32[16,32,256]{2,1,0:T(8,128)S(1)}, u32[]{:S(2)}, u32[]{:S(2)}) %all-to-all-start.1) | async-done | bytes 524320 | tf_op jit(solution)/shard_map/all_to_all | solution.py:56
  33.2 0.0 copy-start.2
  33.2 0.3 fusion.12
  33.4 0.0 copy-start.1
  33.5 0.0 copy-start.4
  33.5 0.0 collective-permute-done
  33.5 0.6 %copy-done.2 = f32[128,256]{1,0:T(8,128)S(1)} copy-done((f32[128,256]{1,0:T(8,128)S(1)}, f32[128,256]{1,0:T(8,128)}, u32[]{:S(2)}) %copy-start.2) | copy-done | bytes 131096
  34.1 0.2 fusion.2
  34.3 0.1 copy-done.1
  34.4 0.0 copy-done.4
  34.4 0.9 %fusion = f32[128,256]{1,0:T(8,128)} fusion(f32[128,256]{1,0:T(8,128)S(1)} %fusion.2, f32[256,256]{1,0:T(8,128)S(1)} %copy-done.1, f32[256]{0:T(256)S(1)} %copy-done.4), kind=kOutput, calls=%fused_computation.2 | convolution fusion | flops 50397184 | bytes 525312 | tf_op jit(solution)/shard_map/dot_general | solution.py:8
  (7 shorter events, 0.0 us)
Async XLA Ops:
  0.0 13.9 %copy-start = (f32[512,256]{1,0:T(8,128)S(1)}, f32[512,256]{1,0:T(8,128)}, u32[]{:S(2)}) copy-start(f32[512,256]{1,0:T(8,128)} %param.8) | copy-start | bytes 1572868
  0.0 13.9 %all-to-all-start = ((s32[16,1,32]{2,1,0:T(1,128)}), s32[16,1,32]{2,1,0:T(1,128)S(1)}, u32[]{:S(2)}, u32[]{:S(2)}) async-start(s32[16,1,32]{2,1,0:T(1,128)} %bitcast.44), calls=%async_computation | async-start | bytes 16384 | tf_op jit(solution)/shard_map/all_to_all | solution.py:26
  7.6 0.7 %copy-start.3 = (s32[128,15]{0,1:T(8,128)S(1)}, s32[128,15]{0,1:T(8,128)}, u32[]{:S(2)}) copy-start(s32[128,15]{0,1:T(8,128)} %param.13) | copy-start | bytes 23044
  8.3 0.7 %copy-start.5 = (s32[16]{0:T(128)S(1)}, s32[16]{0:T(128)}, u32[]{:S(2)}) copy-start(s32[16]{0:T(128)} %param.12) | copy-start | bytes 196
  15.2 3.7 %copy-start.6 = (s32[128]{0:T(128)S(1)}, s32[128]{0:T(128)}, u32[]{:S(2)}) copy-start(s32[128]{0:T(128)} %param.10) | copy-start | bytes 1540
  15.2 17.9 %all-to-all-start.1 = ((f32[16,32,256]{2,1,0:T(8,128)}), f32[16,32,256]{2,1,0:T(8,128)S(1)}, u32[]{:S(2)}, u32[]{:S(2)}) async-start(f32[16,32,256]{2,1,0:T(8,128)} %fusion.3), calls=%async_computation.1 | async-start | bytes 1048576 | tf_op jit(solution)/shard_map/all_to_all | solution.py:56
  19.7 13.8 %collective-permute-start = (f32[128,256]{1,0:T(8,128)S(1)}, f32[128,256]{1,0:T(8,128)S(1)}, u32[]{:S(2)}, u32[]{:S(2)}) collective-permute-start(f32[128,256]{1,0:T(8,128)S(1)} %gather_fusion), channel_id=1, source_target_pairs={{0,16},{16,0},{1,17},{17,1},{2,18},{18,2},{3,19},{19,3},{4,20},{20... | collective-permute-start | bytes 393224 | tf_op jit(solution)/shard_map/ppermute | solution.py:32
  33.2 0.9 %copy-start.2 = (f32[128,256]{1,0:T(8,128)S(1)}, f32[128,256]{1,0:T(8,128)}, u32[]{:S(2)}) copy-start(f32[128,256]{1,0:T(8,128)} %param.9) | copy-start | bytes 393220
  33.4 1.0 %copy-start.1 = (f32[256,256]{1,0:T(8,128)S(1)}, f32[256,256]{1,0:T(8,128)}, u32[]{:S(2)}) copy-start(f32[256,256]{1,0:T(8,128)} %param.14) | copy-start | bytes 786436
  33.5 1.0 %copy-start.4 = (f32[256]{0:T(256)S(1)}, f32[256]{0:T(256)}, u32[]{:S(2)}) copy-start(f32[256]{0:T(256)} %param.15) | copy-start | bytes 3076
